TPU v7x, 32 devices: a whole 2x2x4 slice. The times are simulated.
32 devices in a mesh: groups: 1, row: 4 (over z), col: 4 (over y, x), ksplit: 2 (over core).
Axes of the slice: x: 2, y: 2, z: 4, core: 2. Of those that a mesh axis runs over, the one named last changes fastest.
Arguments:
- pair_state: bfloat16 [128, 128, 128], P(('groups', 'row'), ('col', 'ksplit')), may hold values from -6 to 6
- residue_mask: int32 [128], P('groups'), may hold values 0 or 1
- input_gain: float32 [128], replicated, may hold values from 0.1 to 1.9
- input_shift: float32 [128], replicated, may hold values from -3 to 3
- left_right: bfloat16 [128, 512], replicated, may hold values from -0.5 to 0.5
- output_gate: bfloat16 [128, 128], replicated, may hold values from -0.5 to 0.5
- final_gain: float32 [128], replicated, may hold values from 0.1 to 1.9
- final_shift: float32 [128], replicated, may hold values from -3 to 3
- output_weight: bfloat16 [128, 128], replicated, may hold values from -0.5 to 0.5
Outputs:
- pair_update: bfloat16 [128, 128, 128], P(('groups', 'row'), ('col', 'ksplit'))
All inputs are finite; a program needn't handle non-finite values.
Results may differ from a plain program's by a relative error of at most 0.0053.
Values may be sent and summed in bfloat16 or wider, within the bound.
A program may use at most 64 MiB of HBM per device.

v0:
```python
import functools

import jax
import jax.numpy as jnp
from jax import lax
from jax.experimental import pallas as pl
from jax.experimental.pallas import tpu as pltpu
from jax.sharding import PartitionSpec as P

MESH = pl.DeviceIdType.MESH
LANES = 128
F32 = jnp.float32
BF16 = jnp.bfloat16
BACK = jnp.bfloat16


def norm_rows(data, gain, shift):
    average = jnp.mean(data, axis=-1, keepdims=True)
    centred = data - average
    spread = jnp.mean(centred * centred, axis=-1, keepdims=True)
    return centred * lax.rsqrt(spread + 1e-05) * gain + shift


def swap_blocks(parts, width):
    count = len(parts)
    lane_block = lax.broadcasted_iota(jnp.int32, parts[0].shape, 1) // width
    parts = list(parts)
    step = count // 2
    while step:
        upper = (lane_block & step) != 0
        for low in range(count):
            if low & step:
                continue
            first, second = parts[low], parts[low + step]
            parts[low] = jnp.where(upper, pltpu.roll(second, step * width, 1), first)
            parts[low + step] = jnp.where(
                upper, second, pltpu.roll(first, LANES - step * width, 1)
            )
        step //= 2
    return parts


def kernel(sizes, *refs):
    row_count, col_count, split_count, tile_rows, tile_cols, channels, hidden = sizes
    hbm_inputs, out_ref, inputs = refs[:9], refs[9], refs[10:19]
    normed_buf, gate_buf, left_stage, right_stage = refs[19:23]
    left_send, right_send, left_recv, right_recv, back, home = refs[23:29]
    load_sem, left_out, left_in, right_out, right_in, back_out, back_in = refs[29:36]
    state_ref, mask_ref, input_gain, input_shift, left_right = inputs[:5]
    output_gate, final_gain, final_shift, output_weight = inputs[5:]
    plane = col_count * split_count
    devices = row_count * plane
    owners = devices // 2
    half_rows = row_count // 2
    blocks = LANES // tile_rows
    my_row = lax.axis_index("row")
    my_plane = lax.axis_index("col") * split_count + lax.axis_index("ksplit")
    me = my_row * plane + my_plane
    my_base = (my_row // half_rows) * owners
    my_group = lax.rem(me, owners)
    my_inner = lax.rem(my_row, half_rows)

    def place(index):
        within = lax.rem(index, plane)
        return {
            "row": index // plane,
            "col": within // split_count,
            "ksplit": lax.rem(within, split_count),
        }

    loads = [
        pltpu.make_async_copy(source, target, load_sem.at[at])
        for at, (source, target) in enumerate(zip(hbm_inputs, inputs))
    ]
    for load in loads:
        load.start()

    barrier = pltpu.get_barrier_semaphore()

    def greet(step, carry):
        pl.semaphore_signal(
            barrier, inc=1, device_id=place(lax.rem(me + step, devices)), device_id_type=MESH
        )
        return carry

    lax.fori_loop(1, devices, greet, 0)
    for load in loads:
        load.wait()

    positions = tile_rows * tile_cols
    state = state_ref[...].astype(F32).reshape(positions, channels)
    normed = norm_rows(state, input_gain[...], input_shift[...]).astype(BF16)
    normed_buf[...] = normed.astype(F32)
    weights = jnp.transpose(left_right[...].astype(F32)).astype(BF16)

    lane = lax.broadcasted_iota(jnp.int32, (1, LANES), 1)
    lane_block = lax.broadcasted_iota(jnp.int32, (tile_rows, LANES), 1) // tile_rows
    mask_line = mask_ref[...].astype(F32)
    mask_rows = jnp.broadcast_to(mask_line, (tile_rows, LANES))
    row_live = mask_rows
    turn = lax.rem(lane_block - my_row + row_count, row_count)
    for shift in range(1, blocks):
        row_live = jnp.where(turn == shift, pltpu.roll(mask_rows, shift * tile_rows, 1), row_live)

    lives, packs = [], []
    for quarter in range(tile_cols // blocks):
        rows = []
        col_live = jnp.zeros((tile_rows, LANES), F32)
        for inner in range(blocks):
            k = quarter * blocks + inner
            rows.append(normed_buf[pl.ds(k, tile_rows, stride=tile_cols), :])
            alive = jnp.where(lane == my_plane * tile_cols + k, mask_line, 0.0)
            alive = jnp.sum(alive, axis=1, keepdims=True)
            col_live = jnp.where(lane_block == inner, alive, col_live)
        lives.append(row_live * col_live)
        packs.append(jnp.concatenate(rows, axis=0).astype(BF16))

    def make_side(side, stage, ready):
        own = weights[side * 2 * hidden : (side + 1) * 2 * hidden]
        for quarter in range(tile_cols // blocks):
            projected = lax.dot_general(
                own, packs[quarter], (((1,), (1,)), ((), ())), preferred_element_type=F32
            )
            parts = []
            for block in range(blocks):
                at = block * tile_rows
                value = projected[at : at + tile_rows]
                gate = projected[at + hidden : at + hidden + tile_rows]
                parts.append(lives[quarter] * jax.nn.sigmoid(gate) * value)
            swapped = swap_blocks(parts, tile_rows)
            for inner in range(blocks):
                k = quarter * blocks + inner
                stage[pl.ds(k, tile_rows, stride=tile_cols), :] = swapped[inner]
        ready[...] = stage[...].reshape(ready.shape).astype(BF16)

    make_side(1, right_stage, right_send)
    pl.semaphore_wait(barrier, devices - 1)

    def right_copy(target, source, arriving):
        row = source // plane
        return pltpu.make_async_remote_copy(
            src_ref=right_send.at[:, lax.rem(target, owners)],
            dst_ref=right_recv.at[:, row, lax.rem(source, plane)],
            send_sem=right_out.at[target],
            recv_sem=right_in.at[source],
            device_id=place(source if arriving else target),
            device_id_type=MESH,
        )

    def left_copy(target, source, arriving):
        row = lax.rem(source, owners) // plane
        return pltpu.make_async_remote_copy(
            src_ref=left_send.at[:, target],
            dst_ref=left_recv.at[:, row, lax.rem(source, plane)],
            send_sem=left_out.at[target],
            recv_sem=left_in.at[lax.rem(source, owners)],
            device_id=place(my_base + (lax.rem(source, owners) if arriving else target)),
            device_id_type=MESH,
        )

    def back_copy(target, source, arriving):
        return pltpu.make_async_remote_copy(
            src_ref=back.at[target],
            dst_ref=home.at[source],
            send_sem=back_out.at[target],
            recv_sem=back_in.at[source],
            device_id=place(my_base + (source if arriving else target)),
            device_id_type=MESH,
        )

    far_base = owners - my_base

    def send_far(step, carry):
        right_copy(far_base + lax.rem(my_group + step, owners), me, False).start()
        return carry

    def send_near(step, carry):
        right_copy(my_base + lax.rem(my_group + step, owners), me, False).start()
        return carry

    def send_left(step, carry):
        left_copy(lax.rem(my_group + step, owners), me, False).start()
        return carry

    lax.fori_loop(0, owners, send_far, 0)
    lax.fori_loop(1, owners, send_near, 0)
    right_recv[:, my_row, my_plane] = right_send[:, my_group]
    make_side(0, left_stage, left_send)
    lax.fori_loop(1, owners, send_left, 0)
    left_recv[:, my_inner, my_plane] = left_send[:, my_group]
    gates = jnp.dot(normed, output_gate[...], preferred_element_type=F32)
    gate_buf[...] = jax.nn.sigmoid(gates)

    def wait_left(step, carry):
        source = lax.rem(my_group + owners - step, owners)
        left_copy(source, source, True).wait_recv()
        return carry

    lax.fori_loop(1, owners, wait_left, 0)

    depth = plane * tile_cols
    half_bit = (lax.broadcasted_iota(jnp.int32, (tile_rows, LANES), 1) // tile_cols) & 1
    lefts = []
    for bit in range(2):
        both = [
            jnp.transpose(left_recv[bit, inner].reshape(depth, LANES).astype(F32))
            for inner in range(half_rows)
        ]
        lefts.append(jnp.concatenate(both, axis=0).astype(BF16))

    for turn in range(row_count):
        if turn < half_rows:
            row = my_base // plane + lax.rem(my_inner + turn, half_rows)
        else:
            row = far_base // plane + lax.rem(my_inner + turn, half_rows)

        def wait_right(step, carry):
            source = row * plane + lax.rem(my_plane + step, plane)
            right_copy(source, source, True).wait_recv()
            return carry

        lax.fori_loop(1 if turn == 0 else 0, plane, wait_right, 0)
        products = [
            jnp.dot(
                lefts[bit], right_recv[bit, row].reshape(depth, LANES), preferred_element_type=F32
            )
            for bit in range(2)
        ]
        for inner in range(half_rows):
            mixed = []
            for product in products:
                piece = product[inner * LANES : (inner + 1) * LANES]
                chosen = piece[:tile_rows]
                for block in range(1, blocks):
                    chosen = jnp.where(
                        lane_block == block,
                        piece[block * tile_rows : (block + 1) * tile_rows],
                        chosen,
                    )
                mixed.append(chosen)
            first = jnp.where(half_bit == 0, mixed[0], pltpu.roll(mixed[1], tile_cols, 1))
            second = jnp.where(
                half_bit == 1, mixed[1], pltpu.roll(mixed[0], LANES - tile_cols, 1)
            )
            for half, part in ((0, first), (1, second)):
                target = inner * plane + row * 2 + half
                back[target] = part.astype(BACK)

                @pl.when(target != my_group)
                def _():
                    back_copy(target, my_group, False).start()

                @pl.when(target == my_group)
                def _():
                    home[my_group] = back[my_group]

    def wait_back(step, carry):
        source = lax.rem(my_group + owners - step, owners)
        back_copy(source, source, True).wait_recv()
        return carry

    lax.fori_loop(1, owners, wait_back, 0)

    left_stage[...] = home[...].astype(F32).reshape(owners * tile_rows, LANES)
    step_rows = LANES // tile_cols
    for group in range(tile_rows // step_rows):
        rows = [
            left_stage[pl.ds(group * step_rows + at, owners, stride=tile_rows), :]
            for at in range(step_rows)
        ]
        turned = jnp.transpose(jnp.concatenate(rows, axis=0))
        parts = [turned[b * tile_cols : (b + 1) * tile_cols] for b in range(step_rows)]
        together = jnp.concatenate(swap_blocks(parts, owners), axis=0)
        normed_out = norm_rows(together, final_gain[...], final_shift[...]).astype(BF16)
        projected_out = jnp.dot(normed_out, output_weight[...], preferred_element_type=F32)
        gated = gate_buf[group * LANES : (group + 1) * LANES] * projected_out
        out_ref[group * step_rows : (group + 1) * step_rows] = gated.reshape(
            step_rows, tile_cols, channels
        ).astype(BF16)

    def drain_near(step, carry):
        target = lax.rem(my_group + step, owners)
        right_copy(my_base + target, me, False).wait_send()
        left_copy(target, me, False).wait_send()
        back_copy(target, my_group, False).wait_send()
        return carry

    def drain_far(step, carry):
        right_copy(far_base + lax.rem(my_group + step, owners), me, False).wait_send()
        return carry

    lax.fori_loop(1, owners, drain_near, 0)
    lax.fori_loop(0, owners, drain_far, 0)


def fused(sizes, *arrays):
    row_count, col_count, split_count, tile_rows, tile_cols, channels, hidden = sizes
    plane = col_count * split_count
    devices = row_count * plane
    owners = devices // 2
    state, *lines, weights, gate, gain_out, shift_out, weight_out = arrays
    lines = [line[None] for line in lines]
    operands = [state, *lines, weights, gate, gain_out[None], shift_out[None], weight_out]
    flat = (tile_rows * tile_cols, LANES)
    tile = (tile_cols, LANES)
    counts = (len(operands), owners, owners, devices, devices, owners, owners)
    return pl.pallas_call(
        functools.partial(kernel, sizes),
        out_shape=pltpu.VMEM(state.shape, BF16),
        in_specs=[pl.BlockSpec(memory_space=pl.ANY)] * len(operands),
        out_specs=pl.BlockSpec(memory_space=pltpu.VMEM),
        scratch_shapes=[pltpu.VMEM(item.shape, item.dtype) for item in operands]
        + [pltpu.VMEM(flat, F32)] * 4
        + [pltpu.VMEM((2, owners) + tile, BF16)] * 2
        + [
            pltpu.VMEM((2, row_count // 2, plane) + tile, BF16),
            pltpu.VMEM((2, row_count, plane) + tile, BF16),
            pltpu.VMEM((owners, tile_rows, LANES), BACK),
            pltpu.VMEM((owners, tile_rows, LANES), BACK),
        ]
        + [pltpu.SemaphoreType.DMA((count,)) for count in counts],
        compiler_params=pltpu.CompilerParams(collective_id=0, has_side_effects=True),
    )(*operands)


def update(*arrays):
    state, mask, weight_out = arrays[0], arrays[1], arrays[8]
    tile_rows, tile_cols, channels = state.shape
    hidden = weight_out.shape[0]
    row_count, col_count = lax.axis_size("row"), lax.axis_size("col")
    split_count = lax.axis_size("ksplit")
    devices = row_count * col_count * split_count
    fits = (
        channels == LANES
        and hidden == LANES
        and mask.shape[0] == LANES
        and row_count * tile_rows == LANES
        and devices == tile_rows
        and row_count % 2 == 0
        and devices // 2 == tile_cols
        and tile_rows == 2 * tile_cols
        and tile_cols % 16 == 0
    )
    if fits:
        sizes = (row_count, col_count, split_count, tile_rows, tile_cols, channels, hidden)
        return fused(sizes, *arrays)
    return body(*arrays)


def norm_over(data, norm_gain, norm_shift, over_axis):
    average = jnp.mean(data, axis=over_axis, keepdims=True)
    centred = data - average
    spread = jnp.mean(centred * centred, axis=over_axis, keepdims=True)
    return centred * lax.rsqrt(spread + 1e-05) * norm_gain + norm_shift


def gated_side(normed_in, weights, live_mask, hidden):
    values = jnp.einsum(
        "ikc,ch->hik", normed_in, weights[:, :hidden], preferred_element_type=jnp.float32
    )
    gates = jnp.einsum(
        "ikc,ch->hik", normed_in, weights[:, hidden:], preferred_element_type=jnp.float32
    )
    return (live_mask * jax.nn.sigmoid(gates) * values).astype(jnp.bfloat16)


def contract_parts(left_parts, right_parts, row_count, col_count):
    count_items = left_parts.shape[2]
    tile_rows = left_parts.shape[3]
    tile_cols = left_parts.shape[4]

    def assemble(parts):
        return parts.transpose(2, 0, 3, 1, 4).reshape(
            count_items, row_count * tile_rows, col_count * tile_cols
        )

    products = jnp.einsum(
        "cik,cjk->cij",
        assemble(left_parts),
        assemble(right_parts),
        preferred_element_type=jnp.float32,
    )
    returned = products.reshape(count_items, row_count, tile_rows, col_count, tile_cols)
    return returned.transpose(1, 3, 0, 2, 4)


def body(
    pair_state,
    residue_mask,
    input_gain,
    input_shift,
    left_right,
    output_gate,
    final_gain,
    final_shift,
    output_weight,
):
    tile_rows, tile_cols, channels = pair_state.shape
    hidden = output_weight.shape[0]
    normed_in = norm_over(pair_state.astype(jnp.float32), input_gain, input_shift, 2).astype(
        jnp.bfloat16
    )
    row_start = lax.axis_index("row") * tile_rows
    col_start = lax.axis_index(("col", "ksplit")) * tile_cols
    row_live = lax.dynamic_slice_in_dim(residue_mask, row_start, tile_rows).astype(jnp.float32)
    col_live = lax.dynamic_slice_in_dim(residue_mask, col_start, tile_cols).astype(jnp.float32)
    live_mask = row_live[:, None] * col_live[None, :]
    left_side = gated_side(normed_in, left_right[:, : 2 * hidden], live_mask, hidden)
    right_side = gated_side(normed_in, left_right[:, 2 * hidden :], live_mask, hidden)
    devices_all = lax.axis_size(("row", "col", "ksplit"))
    row_count = lax.axis_size("row")
    col_count = devices_all // row_count
    per_device = hidden // devices_all
    grouped_left = left_side.reshape(devices_all, per_device, tile_rows, tile_cols)
    grouped_right = right_side.reshape(devices_all, per_device, tile_rows, tile_cols)
    left_parts = lax.all_to_all(
        grouped_left, ("row", "col", "ksplit"), split_axis=0, concat_axis=0, tiled=True
    )
    right_parts = lax.all_to_all(
        grouped_right, ("row", "col", "ksplit"), split_axis=0, concat_axis=0, tiled=True
    )
    count_items = left_parts.shape[1]
    shaped_left = left_parts.reshape(row_count, col_count, count_items, tile_rows, tile_cols)
    shaped_right = right_parts.reshape(row_count, col_count, count_items, tile_rows, tile_cols)
    returned = contract_parts(shaped_left, shaped_right, row_count, col_count)
    returned = returned.reshape(devices_all, count_items, tile_rows, tile_cols)
    received = lax.all_to_all(
        returned, ("row", "col", "ksplit"), split_axis=0, concat_axis=0, tiled=True
    )
    mixed_tile = received.reshape(hidden, tile_rows, tile_cols)
    normed_out = norm_over(
        mixed_tile, final_gain[:, None, None], final_shift[:, None, None], 0
    ).astype(jnp.bfloat16)
    projected_out = jnp.einsum(
        "hij,hc->ijc", normed_out, output_weight, preferred_element_type=jnp.float32
    )
    gate_values = jax.nn.sigmoid(
        jnp.einsum("ijc,cd->ijd", normed_in, output_gate, preferred_element_type=jnp.float32)
    )
    return (gate_values * projected_out).astype(jnp.bfloat16)


def solution(mesh):
    placed = (
        P(("groups", "row"), ("col", "ksplit"), None),
        P("groups"),
        P(),
        P(),
        P(),
        P(),
        P(),
        P(),
        P(),
    )
    return jax.shard_map(
        update,
        mesh=mesh,
        in_specs=placed,
        out_specs=P(("groups", "row"), ("col", "ksplit"), None),
        check_vma=False,
    )
```

profile of v0, /device:TPU:0, one launch (start us, length us, event | category | flops | bytes accessed | tf_op | source)
XLA Modules:
  0.0 22.9 jit_solution(9343367676868543208)
XLA Ops:
  0.0 22.2 %shard_map.91 = bf16[32,16,128]{2,1,0:T(8,128)(2,1)S(1)} custom-call(bf16[32,16,128]{2,1,0:T(8,128)(2,1)} %refs_0_.1, s32[1,128]{1,0:T(1,128)} %bitcast.5, f32[1,128]{1,0:T(1,128)} %bitcast.6, f32[1,128]{1,0:T(1,128)} %bitcast.7, bf16[128,512]{1,0:T(8,128)(2,1)} %refs_4_.1, bf16[128,128]{1,0:T(8,128)(2,1)} %refs_5_.1, f32[1,128]{1,0:T(1,128)} %bitcast.8, ...), custom_call_target="tpu_custom_call" | custom-call | tf_op jit(solution)/shard_map/pallas_call | solution.py:307
  22.2 0.7 %copy.11 = bf16[32,16,128]{2,1,0:T(8,128)(2,1)} copy(bf16[32,16,128]{2,1,0:T(8,128)(2,1)S(1)} %shard_map.91) | data formatting | bytes 262144
where the time goes:
time: 23 us; the launch traced here: 22.9 us
  Pallas kernels  22.2 us (97%)
  local copies, waits for them, and re-layouts  0.66 us (3%)
    pallas_call x1, Pallas kernels, fused(): pl.pallas_call(functools.partial(kernel, sizes), out_shape=pltpu.VMEM(sta...  22.2 us
    unnamed x1, local copies, waits for them, and re-layouts  0.66 us

commit v1 on v0

--- a/solution.py
+++ b/solution.py
@@ -44,53 +44,73 @@
     row_count, col_count, split_count, tile_rows, tile_cols, channels, hidden = sizes
     hbm_inputs, out_ref, inputs = refs[:9], refs[9], refs[10:19]
     normed_buf, gate_buf, left_stage, right_stage = refs[19:23]
-    left_send, right_send, left_recv, right_recv, back, home = refs[23:29]
-    load_sem, left_out, left_in, right_out, right_in, back_out, back_in = refs[29:36]
+    left_send, right_send, left_recv, right_recv, pieces = refs[23:28]
+    load_sem, sent_sem, left_in, right_in, back_in, cross_sem, far_sem = refs[28:35]
     state_ref, mask_ref, input_gain, input_shift, left_right = inputs[:5]
     output_gate, final_gain, final_shift, output_weight = inputs[5:]
     plane = col_count * split_count
-    devices = row_count * plane
-    owners = devices // 2
+    owners = plane * row_count // 2
     half_rows = row_count // 2
     blocks = LANES // tile_rows
+    home, back = pieces.at[pl.ds(0, owners)], pieces.at[pl.ds(owners, owners)]
     my_row = lax.axis_index("row")
     my_plane = lax.axis_index("col") * split_count + lax.axis_index("ksplit")
-    me = my_row * plane + my_plane
-    my_base = (my_row // half_rows) * owners
-    my_group = lax.rem(me, owners)
+    my_half = my_row // half_rows
     my_inner = lax.rem(my_row, half_rows)
-
-    def place(index):
-        within = lax.rem(index, plane)
+    my_group = my_inner * plane + my_plane
+    first_row = my_half * half_rows
+    near_row = first_row + 1 - my_inner
+    far_close = half_rows - my_half
+    far_last = (row_count - 1) * (1 - my_half)
+
+    def place(row, position):
         return {
-            "row": index // plane,
-            "col": within // split_count,
-            "ksplit": lax.rem(within, split_count),
+            "row": row,
+            "col": position // split_count,
+            "ksplit": lax.rem(position, split_count),
         }
+
+    def peer(step):
+        return lax.rem(my_plane + step, plane)
 
     loads = [
         pltpu.make_async_copy(source, target, load_sem.at[at])
         for at, (source, target) in enumerate(zip(hbm_inputs, inputs))
     ]
-    for load in loads:
-        load.start()
+    for at in (0, 2, 3, 4, 1, 5, 8, 6, 7):
+        loads[at].start()
 
     barrier = pltpu.get_barrier_semaphore()
 
-    def greet(step, carry):
+    def greet(row, position):
         pl.semaphore_signal(
-            barrier, inc=1, device_id=place(lax.rem(me + step, devices)), device_id_type=MESH
+            barrier, inc=1, device_id=place(row, position), device_id_type=MESH
         )
-        return carry
-
-    lax.fori_loop(1, devices, greet, 0)
-    for load in loads:
-        load.wait()
+
+    for step in range(1, plane):
+        greet(my_row, peer(step))
+    greet(near_row, my_plane)
+
+    @pl.when(my_half == 0)
+    def _():
+        for row in range(half_rows, row_count):
+            for step in range(plane):
+                greet(row, peer(step))
+
+    def tell(sem, row):
+        pl.semaphore_signal(
+            sem, inc=1, device_id=place(row, my_plane), device_id_type=MESH
+        )
+
+    for at in (0, 2, 3):
+        loads[at].wait()
 
     positions = tile_rows * tile_cols
     state = state_ref[...].astype(F32).reshape(positions, channels)
     normed = norm_rows(state, input_gain[...], input_shift[...]).astype(BF16)
     normed_buf[...] = normed.astype(F32)
+    loads[4].wait()
+    loads[1].wait()
     weights = jnp.transpose(left_right[...].astype(F32)).astype(BF16)
 
     lane = lax.broadcasted_iota(jnp.int32, (1, LANES), 1)
@@ -133,70 +153,80 @@
                 stage[pl.ds(k, tile_rows, stride=tile_cols), :] = swapped[inner]
         ready[...] = stage[...].reshape(ready.shape).astype(BF16)
 
+    def send_right(row, position):
+        group = lax.rem(row, half_rows) * plane + position
+        pltpu.make_async_remote_copy(
+            src_ref=right_send.at[:, group],
+            dst_ref=right_recv.at[:, my_row, my_plane],
+            send_sem=sent_sem.at[0],
+            recv_sem=right_in.at[my_row],
+            device_id=place(row, position),
+            device_id_type=MESH,
+        ).start()
+
+    def send_left(row, position):
+        group = lax.rem(row, half_rows) * plane + position
+        pltpu.make_async_remote_copy(
+            src_ref=left_send.at[:, group],
+            dst_ref=left_recv.at[:, my_inner, my_plane],
+            send_sem=sent_sem.at[1],
+            recv_sem=left_in.at[my_inner],
+            device_id=place(row, position),
+            device_id_type=MESH,
+        ).start()
+
+    def send_back(inner, position, group):
+        pltpu.make_async_remote_copy(
+            src_ref=back.at[group],
+            dst_ref=home.at[my_group],
+            send_sem=sent_sem.at[2],
+            recv_sem=back_in.at[0],
+            device_id=place(first_row + inner, position),
+            device_id_type=MESH,
+        ).start()
+
+    def wait_bytes(ref, sem):
+        pltpu.make_async_copy(ref, ref, sem).wait()
+
     make_side(1, right_stage, right_send)
-    pl.semaphore_wait(barrier, devices - 1)
-
-    def right_copy(target, source, arriving):
-        row = source // plane
-        return pltpu.make_async_remote_copy(
-            src_ref=right_send.at[:, lax.rem(target, owners)],
-            dst_ref=right_recv.at[:, row, lax.rem(source, plane)],
-            send_sem=right_out.at[target],
-            recv_sem=right_in.at[source],
-            device_id=place(source if arriving else target),
-            device_id_type=MESH,
-        )
-
-    def left_copy(target, source, arriving):
-        row = lax.rem(source, owners) // plane
-        return pltpu.make_async_remote_copy(
-            src_ref=left_send.at[:, target],
-            dst_ref=left_recv.at[:, row, lax.rem(source, plane)],
-            send_sem=left_out.at[target],
-            recv_sem=left_in.at[lax.rem(source, owners)],
-            device_id=place(my_base + (lax.rem(source, owners) if arriving else target)),
-            device_id_type=MESH,
-        )
-
-    def back_copy(target, source, arriving):
-        return pltpu.make_async_remote_copy(
-            src_ref=back.at[target],
-            dst_ref=home.at[source],
-            send_sem=back_out.at[target],
-            recv_sem=back_in.at[source],
-            device_id=place(my_base + (source if arriving else target)),
-            device_id_type=MESH,
-        )
-
-    far_base = owners - my_base
-
-    def send_far(step, carry):
-        right_copy(far_base + lax.rem(my_group + step, owners), me, False).start()
-        return carry
-
-    def send_near(step, carry):
-        right_copy(my_base + lax.rem(my_group + step, owners), me, False).start()
-        return carry
-
-    def send_left(step, carry):
-        left_copy(lax.rem(my_group + step, owners), me, False).start()
-        return carry
-
-    lax.fori_loop(0, owners, send_far, 0)
-    lax.fori_loop(1, owners, send_near, 0)
+    pl.semaphore_wait(barrier, plane + my_half * owners)
+    tell(cross_sem.at[0], near_row)
+
+    @pl.when(my_half == 1)
+    def _():
+        for row in range(half_rows):
+            tell(far_sem.at[my_inner], row)
+        for row in (1, 0):
+            for step in range(plane):
+                send_right(row, peer(step))
+
+    for step in range(1, plane):
+        send_right(my_row, peer(step))
     right_recv[:, my_row, my_plane] = right_send[:, my_group]
     make_side(0, left_stage, left_send)
-    lax.fori_loop(1, owners, send_left, 0)
+    for step in range(1, plane):
+        send_left(my_row, peer(step))
+    pl.semaphore_wait(cross_sem.at[0], 1)
+    for step in range(plane):
+        send_left(near_row, peer(step))
+    for step in range(plane):
+        send_right(near_row, peer(step))
+
     left_recv[:, my_inner, my_plane] = left_send[:, my_group]
+    for at in (5, 8, 6, 7):
+        loads[at].wait()
     gates = jnp.dot(normed, output_gate[...], preferred_element_type=F32)
     gate_buf[...] = jax.nn.sigmoid(gates)
 
-    def wait_left(step, carry):
-        source = lax.rem(my_group + owners - step, owners)
-        left_copy(source, source, True).wait_recv()
-        return carry
-
-    lax.fori_loop(1, owners, wait_left, 0)
+    @pl.when(my_half == 0)
+    def _():
+        for inner in range(half_rows):
+            pl.semaphore_wait(far_sem.at[inner], 1)
+            for step in range(plane):
+                send_right(half_rows + inner, peer(step))
+
+    wait_bytes(left_recv.at[:, my_inner, pl.ds(0, plane - 1)], left_in.at[my_inner])
+    wait_bytes(left_recv.at[:, 1 - my_inner], left_in.at[1 - my_inner])
 
     depth = plane * tile_cols
     half_bit = (lax.broadcasted_iota(jnp.int32, (tile_rows, LANES), 1) // tile_cols) & 1
@@ -208,18 +238,11 @@
         ]
         lefts.append(jnp.concatenate(both, axis=0).astype(BF16))
 
-    for turn in range(row_count):
-        if turn < half_rows:
-            row = my_base // plane + lax.rem(my_inner + turn, half_rows)
+    for row in (my_row, near_row, far_close, far_last):
+        if row is my_row:
+            wait_bytes(right_recv.at[:, row, pl.ds(0, plane - 1)], right_in.at[row])
         else:
-            row = far_base // plane + lax.rem(my_inner + turn, half_rows)
-
-        def wait_right(step, carry):
-            source = row * plane + lax.rem(my_plane + step, plane)
-            right_copy(source, source, True).wait_recv()
-            return carry
-
-        lax.fori_loop(1 if turn == 0 else 0, plane, wait_right, 0)
+            wait_bytes(right_recv.at[:, row], right_in.at[row])
         products = [
             jnp.dot(
                 lefts[bit], right_recv[bit, row].reshape(depth, LANES), preferred_element_type=F32
@@ -243,23 +266,19 @@
                 half_bit == 1, mixed[1], pltpu.roll(mixed[0], LANES - tile_cols, 1)
             )
             for half, part in ((0, first), (1, second)):
-                target = inner * plane + row * 2 + half
-                back[target] = part.astype(BACK)
-
-                @pl.when(target != my_group)
+                position = row * 2 + half
+                group = inner * plane + position
+                back[group] = part.astype(BACK)
+
+                @pl.when(group != my_group)
                 def _():
-                    back_copy(target, my_group, False).start()
-
-                @pl.when(target == my_group)
+                    send_back(inner, position, group)
+
+                @pl.when(group == my_group)
                 def _():
                     home[my_group] = back[my_group]
 
-    def wait_back(step, carry):
-        source = lax.rem(my_group + owners - step, owners)
-        back_copy(source, source, True).wait_recv()
-        return carry
-
-    lax.fori_loop(1, owners, wait_back, 0)
+    wait_bytes(home.at[pl.ds(0, owners - 1)], back_in.at[0])
 
     left_stage[...] = home[...].astype(F32).reshape(owners * tile_rows, LANES)
     step_rows = LANES // tile_cols
@@ -278,32 +297,21 @@
             step_rows, tile_cols, channels
         ).astype(BF16)
 
-    def drain_near(step, carry):
-        target = lax.rem(my_group + step, owners)
-        right_copy(my_base + target, me, False).wait_send()
-        left_copy(target, me, False).wait_send()
-        back_copy(target, my_group, False).wait_send()
-        return carry
-
-    def drain_far(step, carry):
-        right_copy(far_base + lax.rem(my_group + step, owners), me, False).wait_send()
-        return carry
-
-    lax.fori_loop(1, owners, drain_near, 0)
-    lax.fori_loop(0, owners, drain_far, 0)
+    wait_bytes(pieces.at[pl.ds(0, 2 * owners - 1)], sent_sem.at[0])
+    wait_bytes(pieces.at[pl.ds(0, owners - 1)], sent_sem.at[1])
+    wait_bytes(pieces.at[pl.ds(0, owners - 1)], sent_sem.at[2])
 
 
 def fused(sizes, *arrays):
     row_count, col_count, split_count, tile_rows, tile_cols, channels, hidden = sizes
     plane = col_count * split_count
-    devices = row_count * plane
-    owners = devices // 2
+    owners = row_count * plane // 2
     state, *lines, weights, gate, gain_out, shift_out, weight_out = arrays
     lines = [line[None] for line in lines]
     operands = [state, *lines, weights, gate, gain_out[None], shift_out[None], weight_out]
     flat = (tile_rows * tile_cols, LANES)
     tile = (tile_cols, LANES)
-    counts = (len(operands), owners, owners, devices, devices, owners, owners)
+    counts = (len(operands), 3, row_count // 2, row_count, 1)
     return pl.pallas_call(
         functools.partial(kernel, sizes),
         out_shape=pltpu.VMEM(state.shape, BF16),
@@ -315,10 +323,10 @@
         + [
             pltpu.VMEM((2, row_count // 2, plane) + tile, BF16),
             pltpu.VMEM((2, row_count, plane) + tile, BF16),
-            pltpu.VMEM((owners, tile_rows, LANES), BACK),
-            pltpu.VMEM((owners, tile_rows, LANES), BACK),
+            pltpu.VMEM((2 * owners, tile_rows, LANES), BACK),
         ]
-        + [pltpu.SemaphoreType.DMA((count,)) for count in counts],
+        + [pltpu.SemaphoreType.DMA((count,)) for count in counts]
+        + [pltpu.SemaphoreType.REGULAR((count,)) for count in (1, 2)],
         compiler_params=pltpu.CompilerParams(collective_id=0, has_side_effects=True),
     )(*operands)
 
@@ -336,7 +344,7 @@
         and mask.shape[0] == LANES
         and row_count * tile_rows == LANES
         and devices == tile_rows
-        and row_count % 2 == 0
+        and row_count == 4
         and devices // 2 == tile_cols
         and tile_rows == 2 * tile_cols
         and tile_cols % 16 == 0

time: 23 us -> 18.1 us (0.79)
  the two profiles are of different devices: /device:TPU:0 before, /device:TPU:17 now
where the time goes in v1:
time: 18.1 us; the launch traced here: 17.9 us
  Pallas kernels  17.3 us (96%)
  local copies, waits for them, and re-layouts  0.66 us (4%)
    pallas_call x1, Pallas kernels, fused(): pl.pallas_call(functools.partial(kernel, sizes), out_shape=pltpu.VMEM(sta...  17.3 us
    unnamed x1, local copies, waits for them, and re-layouts  0.66 us

profile of v1, /device:TPU:17, one launch (start us, length us, event | category | flops | bytes accessed | tf_op | source)
XLA Modules:
  0.0 17.9 jit_solution(13891573629494312751)
XLA Ops:
  0.0 17.3 %shard_map.91 = bf16[32,16,128]{2,1,0:T(8,128)(2,1)S(1)} custom-call(bf16[32,16,128]{2,1,0:T(8,128)(2,1)} %refs_0_.1, s32[1,128]{1,0:T(1,128)} %bitcast.5, f32[1,128]{1,0:T(1,128)} %bitcast.6, f32[1,128]{1,0:T(1,128)} %bitcast.7, bf16[128,512]{1,0:T(8,128)(2,1)} %refs_4_.1, bf16[128,128]{1,0:T(8,128)(2,1)} %refs_5_.1, f32[1,128]{1,0:T(1,128)} %bitcast.8, ...), custom_call_target="tpu_custom_call" | custom-call | tf_op jit(solution)/shard_map/pallas_call | solution.py:315
  17.3 0.7 %copy.11 = bf16[32,16,128]{2,1,0:T(8,128)(2,1)} copy(bf16[32,16,128]{2,1,0:T(8,128)(2,1)S(1)} %shard_map.91) | data formatting | bytes 262144

commit v2 on v1

--- a/solution.py
+++ b/solution.py
@@ -42,26 +42,26 @@
 
 def kernel(sizes, *refs):
     row_count, col_count, split_count, tile_rows, tile_cols, channels, hidden = sizes
-    hbm_inputs, out_ref, inputs = refs[:9], refs[9], refs[10:19]
-    normed_buf, gate_buf, left_stage, right_stage = refs[19:23]
-    left_send, right_send, left_recv, right_recv, pieces = refs[23:28]
-    load_sem, sent_sem, left_in, right_in, back_in, cross_sem, far_sem = refs[28:35]
-    state_ref, mask_ref, input_gain, input_shift, left_right = inputs[:5]
-    output_gate, final_gain, final_shift, output_weight = inputs[5:]
+    (state_hbm, mask_hbm, input_gain_hbm, input_shift_hbm, left_right_hbm) = refs[:5]
+    (output_gate_hbm, final_gain_hbm, final_shift_hbm, output_weight_hbm) = refs[5:9]
+    out_ref, state_ref, mask_ref, lines, left_right, squares = refs[9:15]
+    normed_buf, normed_wide, gate_buf, left_stage, right_stage, home_stage = refs[15:21]
+    left_send, right_send, left_recv, right_recv, pieces = refs[21:26]
+    load_sem, sent_sem, left_in, right_in, back_in, ready_sem = refs[26:32]
     plane = col_count * split_count
-    owners = plane * row_count // 2
     half_rows = row_count // 2
+    owners = plane * half_rows
     blocks = LANES // tile_rows
+    quarters = tile_cols // blocks
     home, back = pieces.at[pl.ds(0, owners)], pieces.at[pl.ds(owners, owners)]
     my_row = lax.axis_index("row")
     my_plane = lax.axis_index("col") * split_count + lax.axis_index("ksplit")
+    my_col, my_split = lax.axis_index("col"), lax.axis_index("ksplit")
     my_half = my_row // half_rows
     my_inner = lax.rem(my_row, half_rows)
     my_group = my_inner * plane + my_plane
     first_row = my_half * half_rows
     near_row = first_row + 1 - my_inner
-    far_close = half_rows - my_half
-    far_last = (row_count - 1) * (1 - my_half)
 
     def place(row, position):
         return {
@@ -73,12 +73,25 @@
     def peer(step):
         return lax.rem(my_plane + step, plane)
 
-    loads = [
-        pltpu.make_async_copy(source, target, load_sem.at[at])
-        for at, (source, target) in enumerate(zip(hbm_inputs, inputs))
-    ]
-    for at in (0, 2, 3, 4, 1, 5, 8, 6, 7):
-        loads[at].start()
+    def load(source, target, at):
+        pltpu.make_async_copy(source, target, load_sem.at[at]).start()
+
+    def wait_bytes(ref, sem):
+        pltpu.make_async_copy(ref, ref, sem).wait()
+
+    wide = 2 * hidden
+    for at in range(quarters):
+        part = pl.ds(at * (tile_rows // quarters), tile_rows // quarters)
+        load(state_hbm.at[part], state_ref.at[part], 0)
+    load(mask_hbm, mask_ref, 1)
+    load(input_gain_hbm, lines.at[0], 2)
+    load(input_shift_hbm, lines.at[1], 2)
+    load(final_gain_hbm, lines.at[2], 2)
+    load(final_shift_hbm, lines.at[3], 2)
+    load(left_right_hbm.at[:, pl.ds(wide, wide)], left_right.at[1], 4)
+    load(left_right_hbm.at[:, pl.ds(0, wide)], left_right.at[0], 3)
+    load(output_gate_hbm, squares.at[0], 5)
+    load(output_weight_hbm, squares.at[1], 5)
 
     barrier = pltpu.get_barrier_semaphore()
 
@@ -89,30 +102,30 @@
 
     for step in range(1, plane):
         greet(my_row, peer(step))
-    greet(near_row, my_plane)
-
-    @pl.when(my_half == 0)
-    def _():
-        for row in range(half_rows, row_count):
+    for row in range(1, row_count):
+
+        @pl.when(my_row < row)
+        def _():
             for step in range(plane):
                 greet(row, peer(step))
 
-    def tell(sem, row):
-        pl.semaphore_signal(
-            sem, inc=1, device_id=place(row, my_plane), device_id_type=MESH
-        )
-
-    for at in (0, 2, 3):
-        loads[at].wait()
-
-    positions = tile_rows * tile_cols
-    state = state_ref[...].astype(F32).reshape(positions, channels)
-    normed = norm_rows(state, input_gain[...], input_shift[...]).astype(BF16)
-    normed_buf[...] = normed.astype(F32)
-    loads[4].wait()
-    loads[1].wait()
-    weights = jnp.transpose(left_right[...].astype(F32)).astype(BF16)
-
+    def announce():
+        pl.semaphore_wait(barrier, plane - 1 + my_row * plane)
+        for row in range(row_count - 1):
+
+            hears = (my_row > row) & (my_row <= row + half_rows)
+
+            @pl.when(hears & (my_split == split_count - 1))
+            def _():
+                for split in range(split_count):
+                    pl.semaphore_signal(
+                        ready_sem.at[my_row - 1],
+                        inc=1,
+                        device_id={"row": row, "col": my_col, "ksplit": split},
+                        device_id_type=MESH,
+                    )
+
+    wait_bytes(mask_ref, load_sem.at[1])
     lane = lax.broadcasted_iota(jnp.int32, (1, LANES), 1)
     lane_block = lax.broadcasted_iota(jnp.int32, (tile_rows, LANES), 1) // tile_rows
     mask_line = mask_ref[...].astype(F32)
@@ -121,23 +134,38 @@
     turn = lax.rem(lane_block - my_row + row_count, row_count)
     for shift in range(1, blocks):
         row_live = jnp.where(turn == shift, pltpu.roll(mask_rows, shift * tile_rows, 1), row_live)
-
-    lives, packs = [], []
-    for quarter in range(tile_cols // blocks):
-        rows = []
+    lives = []
+    for quarter in range(quarters):
         col_live = jnp.zeros((tile_rows, LANES), F32)
         for inner in range(blocks):
             k = quarter * blocks + inner
-            rows.append(normed_buf[pl.ds(k, tile_rows, stride=tile_cols), :])
             alive = jnp.where(lane == my_plane * tile_cols + k, mask_line, 0.0)
             alive = jnp.sum(alive, axis=1, keepdims=True)
             col_live = jnp.where(lane_block == inner, alive, col_live)
         lives.append(row_live * col_live)
+
+    wait_bytes(lines, load_sem.at[2])
+    wait_bytes(state_ref, load_sem.at[0])
+    positions = tile_rows * tile_cols
+    state = state_ref[...].astype(F32).reshape(positions, channels)
+    normed = norm_rows(state, lines[0], lines[1])
+    normed_wide[...] = normed.astype(BF16)
+    for at in range(tile_rows):
+        normed_buf[pl.ds(at * (tile_cols + 1), tile_cols), :] = normed[
+            at * tile_cols : (at + 1) * tile_cols
+        ]
+    packs = []
+    for quarter in range(quarters):
+        rows = [
+            normed_buf[pl.ds(quarter * blocks + inner, tile_rows, stride=tile_cols + 1), :]
+            for inner in range(blocks)
+        ]
         packs.append(jnp.concatenate(rows, axis=0).astype(BF16))
 
     def make_side(side, stage, ready):
-        own = weights[side * 2 * hidden : (side + 1) * 2 * hidden]
-        for quarter in range(tile_cols // blocks):
+        wait_bytes(left_right.at[side], load_sem.at[3 + side])
+        own = jnp.transpose(left_right[side].astype(F32)).astype(BF16)
+        for quarter in range(quarters):
             projected = lax.dot_general(
                 own, packs[quarter], (((1,), (1,)), ((), ())), preferred_element_type=F32
             )
@@ -150,8 +178,11 @@
             swapped = swap_blocks(parts, tile_rows)
             for inner in range(blocks):
                 k = quarter * blocks + inner
-                stage[pl.ds(k, tile_rows, stride=tile_cols), :] = swapped[inner]
-        ready[...] = stage[...].reshape(ready.shape).astype(BF16)
+                stage[pl.ds(k, tile_rows, stride=tile_cols + 1), :] = swapped[inner]
+        for at in range(tile_rows):
+            ready[at // owners, at % owners] = stage[
+                pl.ds(at * (tile_cols + 1), tile_cols), :
+            ].astype(BF16)
 
     def send_right(row, position):
         group = lax.rem(row, half_rows) * plane + position
@@ -170,7 +201,7 @@
             src_ref=left_send.at[:, group],
             dst_ref=left_recv.at[:, my_inner, my_plane],
             send_sem=sent_sem.at[1],
-            recv_sem=left_in.at[my_inner],
+            recv_sem=left_in.at[0],
             device_id=place(row, position),
             device_id_type=MESH,
         ).start()
@@ -185,48 +216,79 @@
             device_id_type=MESH,
         ).start()
 
-    def wait_bytes(ref, sem):
-        pltpu.make_async_copy(ref, ref, sem).wait()
+    @pl.when(my_col == col_count - 1)
+    def _():
+        announce()
 
     make_side(1, right_stage, right_send)
-    pl.semaphore_wait(barrier, plane + my_half * owners)
-    tell(cross_sem.at[0], near_row)
-
-    @pl.when(my_half == 1)
+    @pl.when(my_col < col_count - 1)
     def _():
-        for row in range(half_rows):
-            tell(far_sem.at[my_inner], row)
-        for row in (1, 0):
-            for step in range(plane):
-                send_right(row, peer(step))
-
-    for step in range(1, plane):
-        send_right(my_row, peer(step))
-    right_recv[:, my_row, my_plane] = right_send[:, my_group]
+        announce()
+
+    pltpu.make_async_copy(
+        right_send.at[:, my_group], right_recv.at[:, my_row, my_plane], right_in.at[my_row]
+    ).start()
+
+    known = {row: set(range(row + 1)) for row in range(row_count)}
+
+    def send_all(own_row, plan):
+        for send, row in plan:
+            if row is None:
+                pl.semaphore_wait(ready_sem.at[half_rows - 1], 1)
+                continue
+            if row not in known[own_row]:
+                known[own_row].add(row)
+                pl.semaphore_wait(ready_sem.at[row - 1], 1)
+            for step in range(1 if row == own_row else 0, plane):
+                send(row, peer(step))
+
+    right, left = send_right, send_left
+    before = {
+        0: (),
+        1: (),
+        2: (),
+        3: (),
+    }
+    after = {
+        0: ((right, 0), (left, 0), (right, 1), (left, 1), (None, None),),
+        1: ((left, 0), (right, 0), (left, 1), (right, 1), (right, 2), (right, 3),),
+        2: ((right, 0), (left, 3), (right, 1), (left, 2), (right, 3), (right, 2),),
+        3: ((left, 2), (right, 0), (right, 1), (left, 3), (right, 2), (right, 3),),
+    }
+
+    for row in range(row_count):
+
+        @pl.when(my_row == row)
+        def _():
+            send_all(row, before[row])
+
     make_side(0, left_stage, left_send)
-    for step in range(1, plane):
-        send_left(my_row, peer(step))
-    pl.semaphore_wait(cross_sem.at[0], 1)
-    for step in range(plane):
-        send_left(near_row, peer(step))
-    for step in range(plane):
-        send_right(near_row, peer(step))
-
-    left_recv[:, my_inner, my_plane] = left_send[:, my_group]
-    for at in (5, 8, 6, 7):
-        loads[at].wait()
-    gates = jnp.dot(normed, output_gate[...], preferred_element_type=F32)
+    pltpu.make_async_copy(
+        left_send.at[:, my_group], left_recv.at[:, my_inner, my_plane], left_in.at[0]
+    ).start()
+    for row in range(row_count):
+
+        @pl.when(my_row == row)
+        def _():
+            send_all(row, after[row])
+
+    wait_bytes(squares, load_sem.at[5])
+    gates = jnp.dot(normed_wide[...], squares[0], preferred_element_type=F32)
     gate_buf[...] = jax.nn.sigmoid(gates)
 
     @pl.when(my_half == 0)
     def _():
-        for inner in range(half_rows):
-            pl.semaphore_wait(far_sem.at[inner], 1)
-            for step in range(plane):
-                send_right(half_rows + inner, peer(step))
-
-    wait_bytes(left_recv.at[:, my_inner, pl.ds(0, plane - 1)], left_in.at[my_inner])
-    wait_bytes(left_recv.at[:, 1 - my_inner], left_in.at[1 - my_inner])
+        wait_bytes(right_recv.at[:, 0], right_in.at[0])
+        pltpu.make_async_remote_copy(
+            src_ref=right_recv.at[:, 0],
+            dst_ref=right_recv.at[:, 0],
+            send_sem=sent_sem.at[3],
+            recv_sem=right_in.at[0],
+            device_id={"row": my_row + half_rows},
+            device_id_type=MESH,
+        ).start()
+
+    wait_bytes(left_recv, left_in.at[0])
 
     depth = plane * tile_cols
     half_bit = (lax.broadcasted_iota(jnp.int32, (tile_rows, LANES), 1) // tile_cols) & 1
@@ -238,11 +300,15 @@
         ]
         lefts.append(jnp.concatenate(both, axis=0).astype(BF16))
 
-    for row in (my_row, near_row, far_close, far_last):
-        if row is my_row:
-            wait_bytes(right_recv.at[:, row, pl.ds(0, plane - 1)], right_in.at[row])
+    for row in range(row_count):
+        if row:
+            wait_bytes(right_recv.at[:, row], right_in.at[row])
         else:
-            wait_bytes(right_recv.at[:, row], right_in.at[row])
+
+            @pl.when(my_half == 1)
+            def _():
+                wait_bytes(right_recv.at[:, 0], right_in.at[0])
+
         products = [
             jnp.dot(
                 lefts[bit], right_recv[bit, row].reshape(depth, LANES), preferred_element_type=F32
@@ -265,8 +331,8 @@
             second = jnp.where(
                 half_bit == 1, mixed[1], pltpu.roll(mixed[0], LANES - tile_cols, 1)
             )
-            for half, part in ((0, first), (1, second)):
-                position = row * 2 + half
+            for core, part in ((0, first), (1, second)):
+                position = row * 2 + core
                 group = inner * plane + position
                 back[group] = part.astype(BACK)
 
@@ -276,28 +342,42 @@
 
                 @pl.when(group == my_group)
                 def _():
-                    home[my_group] = back[my_group]
-
-    wait_bytes(home.at[pl.ds(0, owners - 1)], back_in.at[0])
-
-    left_stage[...] = home[...].astype(F32).reshape(owners * tile_rows, LANES)
+                    pltpu.make_async_copy(
+                        back.at[group], home.at[my_group], back_in.at[0]
+                    ).start()
+
+    wait_bytes(home, back_in.at[0])
+
+    for at in range(owners):
+        home_stage[pl.ds(at * (tile_rows + 1), tile_rows), :] = home[at].astype(F32)
     step_rows = LANES // tile_cols
     for group in range(tile_rows // step_rows):
         rows = [
-            left_stage[pl.ds(group * step_rows + at, owners, stride=tile_rows), :]
+            home_stage[pl.ds(group * step_rows + at, owners, stride=tile_rows + 1), :]
             for at in range(step_rows)
         ]
         turned = jnp.transpose(jnp.concatenate(rows, axis=0))
         parts = [turned[b * tile_cols : (b + 1) * tile_cols] for b in range(step_rows)]
         together = jnp.concatenate(swap_blocks(parts, owners), axis=0)
-        normed_out = norm_rows(together, final_gain[...], final_shift[...]).astype(BF16)
-        projected_out = jnp.dot(normed_out, output_weight[...], preferred_element_type=F32)
+        normed_out = norm_rows(together, lines[2], lines[3]).astype(BF16)
+        projected_out = jnp.dot(normed_out, squares[1], preferred_element_type=F32)
         gated = gate_buf[group * LANES : (group + 1) * LANES] * projected_out
         out_ref[group * step_rows : (group + 1) * step_rows] = gated.reshape(
             step_rows, tile_cols, channels
         ).astype(BF16)
 
-    wait_bytes(pieces.at[pl.ds(0, 2 * owners - 1)], sent_sem.at[0])
+    @pl.when(my_row == 0)
+    def _():
+        wait_bytes(pieces.at[pl.ds(0, owners - 1)], sent_sem.at[0])
+
+    @pl.when(my_row > 0)
+    def _():
+        wait_bytes(pieces.at[pl.ds(0, 2 * owners - 1)], sent_sem.at[0])
+
+    @pl.when(my_half == 0)
+    def _():
+        wait_bytes(right_recv.at[:, 0], sent_sem.at[3])
+
     wait_bytes(pieces.at[pl.ds(0, owners - 1)], sent_sem.at[1])
     wait_bytes(pieces.at[pl.ds(0, owners - 1)], sent_sem.at[2])
 
@@ -310,23 +390,33 @@
     lines = [line[None] for line in lines]
     operands = [state, *lines, weights, gate, gain_out[None], shift_out[None], weight_out]
     flat = (tile_rows * tile_cols, LANES)
+    padded = (tile_rows * (tile_cols + 1), LANES)
     tile = (tile_cols, LANES)
-    counts = (len(operands), 3, row_count // 2, row_count, 1)
     return pl.pallas_call(
         functools.partial(kernel, sizes),
         out_shape=pltpu.VMEM(state.shape, BF16),
         in_specs=[pl.BlockSpec(memory_space=pl.ANY)] * len(operands),
         out_specs=pl.BlockSpec(memory_space=pltpu.VMEM),
-        scratch_shapes=[pltpu.VMEM(item.shape, item.dtype) for item in operands]
-        + [pltpu.VMEM(flat, F32)] * 4
-        + [pltpu.VMEM((2, owners) + tile, BF16)] * 2
-        + [
+        scratch_shapes=[
+            pltpu.VMEM(state.shape, BF16),
+            pltpu.VMEM((1, LANES), jnp.int32),
+            pltpu.VMEM((4, 1, LANES), F32),
+            pltpu.VMEM((2, channels, 2 * hidden), BF16),
+            pltpu.VMEM((2, channels, hidden), BF16),
+            pltpu.VMEM(padded, F32),
+            pltpu.VMEM(flat, BF16),
+            pltpu.VMEM(flat, F32),
+            pltpu.VMEM(padded, F32),
+            pltpu.VMEM(padded, F32),
+            pltpu.VMEM((owners * (tile_rows + 1), LANES), F32),
+            pltpu.VMEM((2, owners) + tile, BF16),
+            pltpu.VMEM((2, owners) + tile, BF16),
             pltpu.VMEM((2, row_count // 2, plane) + tile, BF16),
             pltpu.VMEM((2, row_count, plane) + tile, BF16),
             pltpu.VMEM((2 * owners, tile_rows, LANES), BACK),
         ]
-        + [pltpu.SemaphoreType.DMA((count,)) for count in counts]
-        + [pltpu.SemaphoreType.REGULAR((count,)) for count in (1, 2)],
+        + [pltpu.SemaphoreType.DMA((count,)) for count in (6, 4, 1, row_count, 1)]
+        + [pltpu.SemaphoreType.REGULAR((count,)) for count in (row_count - 1,)],
         compiler_params=pltpu.CompilerParams(collective_id=0, has_side_effects=True),
     )(*operands)
 

time: 18.1 us -> 17.2 us (0.950)
  the two profiles are of different devices: /device:TPU:17 before, /device:TPU:5 now
where the time goes in v2:
time: 17.2 us; the launch traced here: 17.1 us
  Pallas kernels  16.4 us (95%)
  local copies, waits for them, and re-layouts  0.66 us (4%)
    pallas_call x1, Pallas kernels, fused(): pl.pallas_call(functools.partial(kernel, sizes), out_shape=pltpu.VMEM(sta...  16.4 us
    unnamed x1, local copies, waits for them, and re-layouts  0.66 us

profile of v2, /device:TPU:5, one launch (start us, length us, event | category | flops | bytes accessed | tf_op | source)
XLA Modules:
  0.0 17.1 jit_solution(15063693095724444874)
XLA Ops:
  0.0 16.4 %shard_map.91 = bf16[32,16,128]{2,1,0:T(8,128)(2,1)S(1)} custom-call(bf16[32,16,128]{2,1,0:T(8,128)(2,1)} %refs_0_.1, s32[1,128]{1,0:T(1,128)} %bitcast.5, f32[1,128]{1,0:T(1,128)} %bitcast.6, f32[1,128]{1,0:T(1,128)} %bitcast.7, bf16[128,512]{1,0:T(8,128)(2,1)} %refs_4_.1, bf16[128,128]{1,0:T(8,128)(2,1)} %refs_5_.1, f32[1,128]{1,0:T(1,128)} %bitcast.8, ...), custom_call_target="tpu_custom_call" | custom-call | tf_op jit(solution)/shard_map/pallas_call | solution.py:395
  16.4 0.7 %copy.11 = bf16[32,16,128]{2,1,0:T(8,128)(2,1)} copy(bf16[32,16,128]{2,1,0:T(8,128)(2,1)S(1)} %shard_map.91) | data formatting | bytes 262144
